TPU v7x, 32 devices: a whole 2x2x4 slice. The times are simulated.
32 devices in a mesh: island: 16 (over z, y, x), tensor: 2 (over core).
Axes of the slice: x: 2, y: 2, z: 4, core: 2. Of those that a mesh axis runs over, the one named last changes fastest.
Arguments:
- pseudo_grad: float32 [16, 32, 53248], P('island', None, 'tensor'), may hold values from -8000 to 8000
- outer_params: float32 [32, 53248], P('island', 'tensor'), may hold values from -4 to 4
- momentum: float32 [32, 53248], P('island', 'tensor'), may hold values from -6 to 6
- save_pages: int32 [16], replicated, may hold values from 1 to 832, 6656 in all
- writer: int32 [16], replicated, may hold values from 0 to 15, each once
Outputs:
- new_master: float32 [32, 53248], P('island', 'tensor')
- new_momentum: float32 [32, 53248], P('island', 'tensor')
- checkpoint: bfloat16 [16, 832, 256], P('island', None, 'tensor')
Inputs may be any that keep to these rules, and one draw needn't show every extreme that they name: save_pages sums to 6656; the longest range has exactly 832 pages. writer names every island once.
All inputs are finite; a program needn't handle non-finite values.
Results may differ from a plain program's by a relative error of at most 0.0007.
Values may be sent and summed in bfloat16 or wider, within the bound.
A program may use at most 64 MiB of HBM per device.

v0:
```python
import jax
import jax.numpy as jnp
from jax import lax
from jax.sharding import PartitionSpec as P

epsilon = 1e-06
decay_rate = 0.9
outer_rate = 0.7


def body(pseudo_grad, outer_params, momentum, save_pages, writer):
    own_rows = outer_params.shape[0]
    col_width = outer_params.shape[1]
    islands = lax.axis_size("island")
    my_index = lax.axis_index("island")
    own_grad = pseudo_grad[0]
    entries = own_grad.shape[0] * col_width * lax.axis_size("tensor")
    summed = lax.psum(own_grad, "island")
    full_grad = summed / islands
    square_sum = lax.psum(jnp.sum(full_grad * full_grad), "tensor")
    outer_grad = lax.dynamic_slice_in_dim(full_grad, my_index * own_rows, own_rows, 0)
    normed = outer_grad / jnp.sqrt(square_sum / entries + epsilon)
    new_momentum = decay_rate * momentum + normed
    new_master = outer_params - outer_rate * (normed + decay_rate * new_momentum)
    cast_rows = new_master.astype(jnp.bfloat16)
    pages_own = own_rows * col_width // 128
    capacity = 2 * pages_own
    starts = jnp.cumsum(save_pages) - save_pages
    targets = jnp.arange(islands, dtype=jnp.int32)
    owner_table = writer[None, :] == targets[:, None]
    range_start = jnp.sum(jnp.where(owner_table, starts[None, :], 0), axis=1)
    range_length = jnp.sum(jnp.where(owner_table, save_pages[None, :], 0), axis=1)
    is_mine = targets == my_index
    own_start = jnp.sum(jnp.where(is_mine, range_start, 0))
    own_length = jnp.sum(jnp.where(is_mine, range_length, 0))
    slot_ids = jnp.arange(capacity, dtype=jnp.int32)
    own_pages = cast_rows.reshape(pages_own, 128)
    spread_slots = -(-pages_own // islands)
    deliver_slots = -(-capacity // islands)
    spread_ids = jnp.arange(spread_slots, dtype=jnp.int32)
    offset = jnp.mod(targets - my_index * pages_own, islands)
    local_index = offset[:, None] + islands * spread_ids[None, :]
    live_slot = (local_index < pages_own).reshape(-1, 1)
    outgoing = jnp.take(own_pages, jnp.clip(local_index, 0, pages_own - 1).reshape(-1), axis=0)
    outgoing = jnp.where(live_slot, outgoing, jnp.zeros_like(outgoing))
    spread = lax.all_to_all(outgoing, "island", split_axis=0, concat_axis=0, tiled=True)
    deliver_ids = jnp.arange(deliver_slots, dtype=jnp.int32)
    first_page = range_start + jnp.mod(my_index - range_start, islands)
    global_page = first_page[:, None] + islands * deliver_ids[None, :]
    live_out = (global_page < (range_start + range_length)[:, None]).reshape(-1, 1)
    held_index = (
        global_page // pages_own * spread_slots + jnp.mod(global_page, pages_own) // islands
    )
    held_index = jnp.clip(held_index, 0, islands * spread_slots - 1).reshape(-1)
    forward = jnp.take(spread, held_index, axis=0)
    forward = jnp.where(live_out, forward, jnp.zeros_like(forward))
    delivered = lax.all_to_all(forward, "island", split_axis=0, concat_axis=0, tiled=True)
    source = jnp.mod(own_start + slot_ids, islands) * deliver_slots + slot_ids // islands
    source = jnp.clip(source, 0, islands * deliver_slots - 1)
    packed = jnp.take(delivered, source, axis=0)
    packed = jnp.where((slot_ids < own_length)[:, None], packed, jnp.zeros_like(packed))
    return (new_master, new_momentum, packed[None])


def solution(mesh):
    in_specs = (P("island", None, "tensor"), P("island", "tensor"), P("island", "tensor"), P(), P())
    out_specs = (P("island", "tensor"), P("island", "tensor"), P("island", None, "tensor"))
    return jax.shard_map(body, mesh=mesh, in_specs=in_specs, out_specs=out_specs, check_vma=False)
```

profile of v0, /device:TPU:0, one launch (start us, length us, event | category | flops | bytes accessed | tf_op | source)
XLA Modules:
  0.0 218.6 jit_solution(9376555139836277744)
XLA Ops:
  7.2 0.7 all-reduce.2.cloned.1.call-update
  8.0 0.1 min.40
  8.3 0.1 reduce
  8.4 0.1 select_reduce_fusion.1
  8.5 0.7 fusion.32
  9.3 0.1 rem.175
  9.5 0.1 add_compare_fusion
  9.6 0.1 ne.202
  9.8 159.0 %all-reduce.2.cloned.1.call-done = f32[32,26624]{1,0:T(8,128)} async-done(((f32[32,26624]{1,0:T(8,128)}), f32[32,26624]{1,0:T(8,128)}) %all-reduce.2.cloned.1.call-update) | async-done | bytes 3407888 | tf_op jit(solution)/shard_map/psum | solution.py:18
  168.8 3.5 %broadcast_multiply_fusion = (f32[32,26624]{1,0:T(8,128)S(1)}, f32[]{:T(128)}) fusion(f32[32,26624]{1,0:T(8,128)} %all-reduce.2.cloned.1.call-done), kind=kLoop, calls=%fused_computation.4 | loop fusion | flops 2555903 | bytes 6815748 | tf_op jit(solution)/shard_map/div | solution.py:19
  172.2 3.1 %psum.15 = f32[]{:T(128)} all-reduce(f32[]{:T(128)} %get-tuple-element.9), channel_id=1, replica_groups=mesh['island'=16,'tensor'=2] {'tensor'}, use_global_device_ids=true, to_apply=%region_2.0 | all-reduce | flops 1 | bytes 8 | tf_op jit(solution)/shard_map/psum | solution.py:20
  176.0 2.1 fusion.36
  178.2 1.5 gather_fusion
  179.7 0.9 select_select_fusion.1
  180.6 4.7 %all-to-all-start = ((bf16[16,26,128]{2,1,0:T(8,128)(2,1)}), bf16[16,26,128]{2,1,0:T(8,128)(2,1)S(1)}, u32[]{:S(2)}, u32[]{:S(2)}) async-start(bf16[16,26,128]{2,1,0:T(8,128)(2,1)} %select_select_fusion.1), calls=%async_computation | async-start | bytes 262144 | tf_op jit(solution)/shard_map/all_to_all | solution.py:46
  185.4 7.7 %all-to-all-done = bf16[16,26,128]{2,1,0:T(8,128)(2,1)S(1)} async-done(((bf16[16,26,128]{2,1,0:T(8,128)(2,1)}), bf16[16,26,128]{2,1,0:T(8,128)(2,1)S(1)}, u32[]{:S(2)}, u32[]{:S(2)}) %all-to-all-start) | async-done | bytes 106528 | tf_op jit(solution)/shard_map/all_to_all | solution.py:46
  193.1 2.4 %gather_fusion.1 = bf16[832,128]{1,0:T(8,128)(2,1)S(1)} fusion(bf16[416,128]{1,0:T(8,128)(2,1)S(1)} %all_to_all.13, s32[1024]{0:T(1024)S(1)} %pad_clamp_fusion.1), kind=kCustom, calls=%fused_computation.1 | custom fusion | bytes 429312 | tf_op jit(solution)/shard_map/jit(_take)/gather | solution.py:55
  195.5 1.0 select_select_fusion
  196.5 3.5 %all-to-all-start.1 = ((bf16[16,52,128]{2,1,0:T(8,128)(2,1)}), bf16[16,52,128]{2,1,0:T(8,128)(2,1)S(1)}, u32[]{:S(2)}, u32[]{:S(2)}) async-start(bf16[16,52,128]{2,1,0:T(8,128)(2,1)} %select_select_fusion), calls=%async_computation.1 | async-start | bytes 458752 | tf_op jit(solution)/shard_map/all_to_all | solution.py:57
  200.1 0.7 fusion.26
  200.8 1.3 iota_compare_fusion.1
  202.1 6.3 %all-to-all-done.1 = bf16[16,52,128]{2,1,0:T(8,128)(2,1)S(1)} async-done(((bf16[16,52,128]{2,1,0:T(8,128)(2,1)}), bf16[16,52,128]{2,1,0:T(8,128)(2,1)S(1)}, u32[]{:S(2)}, u32[]{:S(2)}) %all-to-all-start.1) | async-done | bytes 213024 | tf_op jit(solution)/shard_map/all_to_all | solution.py:57
  208.4 2.4 %gather_fusion.2 = bf16[832,128]{1,0:T(8,128)(2,1)S(1)} fusion(bf16[832,128]{1,0:T(8,128)(2,1)S(1)} %all_to_all.15, s32[1024]{0:T(1024)S(1)} %pad_clamp_fusion), kind=kCustom, calls=%fused_computation.2 | custom fusion | bytes 429312 | tf_op jit(solution)/shard_map/jit(_take)/gather | solution.py:60
  210.8 1.0 fusion
  (25 shorter events, 0.8 us)
Async XLA Ops:
  7.2 1.0 copy-start
  7.2 1.2 copy-start.1
  7.2 161.6 %all-reduce.2.cloned.1.call-start = ((), (), s32[]{:S(2)}) async-start(), calls=%async_computation.2 | async-start | bytes 6815744 | tf_op jit(solution)/shard_map/psum | solution.py:18
  180.6 12.5 %all-to-all-start = ((bf16[16,26,128]{2,1,0:T(8,128)(2,1)}), bf16[16,26,128]{2,1,0:T(8,128)(2,1)S(1)}, u32[]{:S(2)}, u32[]{:S(2)}) async-start(bf16[16,26,128]{2,1,0:T(8,128)(2,1)} %select_select_fusion.1), calls=%async_computation | async-start | bytes 262144 | tf_op jit(solution)/shard_map/all_to_all | solution.py:46
  196.5 11.8 %all-to-all-start.1 = ((bf16[16,52,128]{2,1,0:T(8,128)(2,1)}), bf16[16,52,128]{2,1,0:T(8,128)(2,1)S(1)}, u32[]{:S(2)}, u32[]{:S(2)}) async-start(bf16[16,52,128]{2,1,0:T(8,128)(2,1)} %select_select_fusion), calls=%async_computation.1 | async-start | bytes 458752 | tf_op jit(solution)/shard_map/all_to_all | solution.py:57
Sparse Core Ops, SparseCore 0:
  13.7 155.0 all-reduce.1
where the time goes:
time: 219 us
  waiting for transfers between devices  174 us (79%)
  between operations  14.9 us (7%)
  other arithmetic  11.8 us (5%)
  starting transfers between devices  8.25 us (4%)
  local copies, waits for them, and re-layouts  6.87 us (3%)
  blocking collectives  3.08 us (1%)
    psum x1, waiting for transfers between devices, body(): summed = lax.psum(own_grad, 'island')  159 us
    all_to_all x1, waiting for transfers between devices, body(): lax.all_to_all(outgoing, 'island', split_axis=0, concat_axis=0, tiled=True)  7.72 us
    all_to_all x1, waiting for transfers between devices, body(): lax.all_to_all(forward, 'island', split_axis=0, concat_axis=0, tiled=True)  6.3 us
    all_to_all x1, starting transfers between devices, body(): lax.all_to_all(outgoing, 'island', split_axis=0, concat_axis=0, tiled=True)  4.69 us
  transfers between devices with their start and end apart: 3, of which 3 were waited for; matrix products, arithmetic and copies ran while one was open for 2% of the time, Pallas kernels for 0%

commit v1 on v0

--- a/solution.py
+++ b/solution.py
@@ -15,7 +15,8 @@
     my_index = lax.axis_index("island")
     own_grad = pseudo_grad[0]
     entries = own_grad.shape[0] * col_width * lax.axis_size("tensor")
-    summed = lax.psum(own_grad, "island")
+    parts = lax.all_gather(own_grad, "island")
+    summed = jnp.sum(parts, axis=0)
     full_grad = summed / islands
     square_sum = lax.psum(jnp.sum(full_grad * full_grad), "tensor")
     outer_grad = lax.dynamic_slice_in_dim(full_grad, my_index * own_rows, own_rows, 0)

time: 219 us -> 628 us (2.87)
  waiting for transfers between devices: 174 us -> 567 us
  other arithmetic: 11.8 us -> 28.8 us
    all_gather x0 -> x1, waiting for transfers between devices: none -> 552 us  [body(): parts = lax.all_gather(own_grad, 'island')]
    psum x1 -> x0, waiting for transfers between devices: 159 us -> none  [body(): summed = lax.psum(own_grad, 'island')]
    reduce_sum x0 -> x1, other arithmetic: none -> 17.3 us  [body(): summed = jnp.sum(parts, axis=0)]
  transfers between devices with their start and end apart: 3 -> 3, of which waited for: 3 -> 3; matrix products, arithmetic and copies ran while one was open for 2% -> 1% of each run, Pallas kernels for 0% -> 0%
where the time goes in v1:
time: 628 us
  waiting for transfers between devices  567 us (90%)
  other arithmetic  28.8 us (5%)
  between operations  14.9 us (2%)
  starting transfers between devices  7.37 us (1%)
  local copies, waits for them, and re-layouts  6.87 us (1%)
    all_gather x1, waiting for transfers between devices, body(): parts = lax.all_gather(own_grad, 'island')  552 us
    reduce_sum x1, other arithmetic, body(): summed = jnp.sum(parts, axis=0)  17.3 us
  transfers between devices with their start and end apart: 3, of which 3 were waited for; matrix products, arithmetic and copies ran while one was open for 1% of the time, Pallas kernels for 0%

profile of v1, /device:TPU:0, one launch (start us, length us, event | category | flops | bytes accessed | tf_op | source)
XLA Modules:
  0.0 627.9 jit_solution(5933027979545774331)
XLA Ops:
  7.2 0.7 all-gather.2.cloned.1.call-update
  8.0 0.1 min.40
  8.3 0.1 reduce
  8.4 0.1 select_reduce_fusion.1
  8.5 0.7 fusion.32
  9.4 0.1 add_compare_fusion
  9.5 0.1 ne.202
  9.7 552.0 %all-gather.2.cloned.1.call-done = f32[16,32,26624]{2,1,0:T(8,128)} async-done(((f32[1,32,26624]{2,1,0:T(8,128)}), f32[16,32,26624]{2,1,0:T(8,128)}) %all-gather.2.cloned.1.call-update) | async-done | bytes 54525968 | tf_op jit(solution)/shard_map/all_gather | solution.py:18
  561.8 17.3 %reduce_sum.54 = f32[32,26624]{1,0:T(8,128)S(1)} reduce(f32[16,32,26624]{2,1,0:T(8,128)} %all-gather.2.cloned.1.call-done, f32[]{:T(128)} %constant.127.clone.1), dimensions={0}, to_apply=%region_0.0 | reduce | flops 12779520 | bytes 57933828 | tf_op jit(solution)/shard_map/reduce_sum | solution.py:19
  579.0 3.1 broadcast_multiply_fusion
  582.2 3.1 psum.7
  586.0 2.3 fusion.36
  588.4 1.5 gather_fusion
  589.9 0.9 select_select_fusion.1
  590.8 3.8 all-to-all-start
  594.6 7.7 %all-to-all-done = bf16[16,26,128]{2,1,0:T(8,128)(2,1)S(1)} async-done(((bf16[16,26,128]{2,1,0:T(8,128)(2,1)}), bf16[16,26,128]{2,1,0:T(8,128)(2,1)S(1)}, u32[]{:S(2)}, u32[]{:S(2)}) %all-to-all-start) | async-done | bytes 106528 | tf_op jit(solution)/shard_map/all_to_all | solution.py:47
  602.4 2.4 gather_fusion.1
  604.8 1.0 select_select_fusion
  605.8 3.5 all-to-all-start.1
  609.3 0.7 fusion.26
  610.0 1.2 iota_compare_fusion.1
  611.2 6.4 %all-to-all-done.1 = bf16[16,52,128]{2,1,0:T(8,128)(2,1)S(1)} async-done(((bf16[16,52,128]{2,1,0:T(8,128)(2,1)}), bf16[16,52,128]{2,1,0:T(8,128)(2,1)S(1)}, u32[]{:S(2)}, u32[]{:S(2)}) %all-to-all-start.1) | async-done | bytes 213024 | tf_op jit(solution)/shard_map/all_to_all | solution.py:58
  617.7 2.4 gather_fusion.2
  620.1 1.0 fusion
  (26 shorter events, 0.9 us)
Async XLA Ops:
  7.2 1.0 copy-start
  7.2 1.2 copy-start.1
  7.2 554.6 %all-gather.2.cloned.1.call-start = ((), (), s32[]{:S(2)}) async-start(), calls=%async_computation.2 | async-start | bytes 57933824 | tf_op jit(solution)/shard_map/all_gather | solution.py:18
  590.8 11.6 %all-to-all-start = ((bf16[16,26,128]{2,1,0:T(8,128)(2,1)}), bf16[16,26,128]{2,1,0:T(8,128)(2,1)S(1)}, u32[]{:S(2)}, u32[]{:S(2)}) async-start(bf16[16,26,128]{2,1,0:T(8,128)(2,1)} %select_select_fusion.1), calls=%async_computation | async-start | bytes 262144 | tf_op jit(solution)/shard_map/all_to_all | solution.py:47
  605.8 11.8 %all-to-all-start.1 = ((bf16[16,52,128]{2,1,0:T(8,128)(2,1)}), bf16[16,52,128]{2,1,0:T(8,128)(2,1)S(1)}, u32[]{:S(2)}, u32[]{:S(2)}) async-start(bf16[16,52,128]{2,1,0:T(8,128)(2,1)} %select_select_fusion), calls=%async_computation.1 | async-start | bytes 458752 | tf_op jit(solution)/shard_map/all_to_all | solution.py:58
Sparse Core Ops, SparseCore 0:
  10.7 551.0 all-gather.1
